TPU v7x, 32 devices: a whole 2x2x4 slice. The times are simulated.
32 devices in a mesh: rep: 2 (over y), fsdp: 16 (over z, x, core).
Axes of the slice: x: 2, y: 2, z: 4, core: 2. Of those that a mesh axis runs over, the one named last changes fastest.
Arguments:
- tokens: bfloat16 [16384, 4096], P(('rep', 'fsdp')), may hold values from -6 to 6
- value_cot: bfloat16 [16384, 1024], P(('rep', 'fsdp')), may hold values from -6 to 6
- value_weight: bfloat16 [2, 4096, 1024], P('rep', 'fsdp'), may hold values from -0.09375 to 0.09375
- global_params: float32 [2097152], P('fsdp'), may hold values from -6 to 6
- local_params: float32 [2, 2097152], P('rep', 'fsdp'), may hold values from -6 to 6
- momentum: float32 [2097152], P('fsdp'), may hold values from -3 to 3
Outputs:
- token_grad: bfloat16 [16384, 4096], P(('rep', 'fsdp'))
- value_grad: float32 [2, 4096, 1024], P('rep', 'fsdp')
- new_global: float32 [2097152], P('fsdp')
- new_moment: float32 [2097152], P('fsdp')
All inputs are finite; a program needn't handle non-finite values.
Results may differ from a plain program's by a relative error of at most 0.001.
Values may be sent and summed in bfloat16 or wider, within the bound.
A program may use at most 128 MiB of HBM per device.

v0:
```python
import jax
import jax.numpy as jnp
from jax import lax
from jax.sharding import PartitionSpec as P


def grad_term(tokens, columns):
    return lax.dot_general(
        tokens, columns, (((0,), (0,)), ((), ())), preferred_element_type=jnp.float32
    )


def shards(tokens, value_cot, value_weight, global_params, local_params, momentum):
    weight = value_weight[0]
    token_grad = lax.dot_general(
        value_cot,
        lax.all_gather(weight, "fsdp", axis=0, tiled=True),
        (((1,), (1,)), ((), ())),
        preferred_element_type=jnp.float32,
    ).astype(jnp.bfloat16)
    groups = lax.axis_size("fsdp")
    factor = 1.0 / jnp.sqrt(jnp.float32(tokens.shape[0] * groups))
    summed = lax.psum_scatter(grad_term(tokens, value_cot), "fsdp", scatter_dimension=0, tiled=True)
    value_grad = (summed * factor)[None]
    totals = lax.psum(local_params[0], "rep")
    pseudo = global_params - totals / lax.axis_size("rep")
    new_moment = 0.9 * momentum + pseudo
    new_global = global_params - 0.7 * (pseudo + 0.9 * new_moment)
    return (token_grad, value_grad, new_global, new_moment)


def solution(mesh):
    in_specs = (
        P(("rep", "fsdp"), None),
        P(("rep", "fsdp"), None),
        P("rep", "fsdp", None),
        P("fsdp"),
        P("rep", "fsdp"),
        P("fsdp"),
    )
    out_specs = (P(("rep", "fsdp"), None), P("rep", "fsdp", None), P("fsdp"), P("fsdp"))
    return jax.shard_map(shards, mesh=mesh, in_specs=in_specs, out_specs=out_specs, check_vma=False)
```

profile of v0, /device:TPU:0, one launch (start us, length us, event | category | flops | bytes accessed | tf_op | source)
XLA Modules:
  0.0 277.8 jit_solution(12506146668002710478)
XLA Ops:
  8.0 0.0 copy-start
  8.0 0.0 all-reduce.2.cloned.1.call-start
  8.1 0.7 all-reduce.2.cloned.1.call-update
  8.7 0.0 all-gather.3.cloned.1.call-start
  8.8 0.5 all-gather.3.cloned.1.call-update
  9.3 0.0 reduce-scatter.2.cloned.1.call-start
  9.4 0.0 copy-done
  9.4 10.6 %fusion.5 = f32[4096,1024]{1,0:T(8,128)} fusion(bf16[512,4096]{1,0:T(8,128)(2,1)} %param.6, bf16[512,1024]{1,0:T(8,128)(2,1)S(1)} %copy-done), kind=kOutput, calls=%fused_computation.7 | convolution fusion | flops 4294967296 | bytes 22020096 | tf_op jit(solution)/shard_map/dot_general | solution.py:8
  20.0 0.0 copy-start.1
  20.0 0.0 copy-start.2
  20.0 0.0 reduce-scatter.2.cloned.1.call-update
  20.0 22.5 %all-reduce.2.cloned.1.call-done = f32[131072]{0:T(1024)} async-done(((f32[131072]{0:T(1024)}), f32[131072]{0:T(1024)}) %all-reduce.2.cloned.1.call-update) | async-done | bytes 524304 | tf_op jit(solution)/shard_map/psum | solution.py:25
  42.5 0.0 copy-done.1
  42.5 0.0 copy-done.2
  42.5 2.1 multiply_subtract_fusion
  44.7 43.5 %all-gather.3.cloned.1.call-done = bf16[1,4096,1024]{2,1,0:T(8,128)(2,1)} async-done(((bf16[1,256,1024]{2,1,0:T(8,128)(2,1)}), bf16[1,4096,1024]{2,1,0:T(8,128)(2,1)}) %all-gather.3.cloned.1.call-update) | async-done | bytes 8388624 | tf_op jit(solution)/shard_map/all_gather | solution.py:17
  88.2 9.5 %fusion.2 = bf16[512,4096]{1,0:T(8,128)(2,1)} fusion(bf16[512,1024]{1,0:T(8,128)(2,1)S(1)} %copy-done, bf16[1,4096,1024]{2,1,0:T(8,128)(2,1)} %all-gather.3.cloned.1.call-done), kind=kOutput, calls=%fused_computation.2 | convolution fusion | flops 4297064448 | bytes 13631488 | tf_op jit(solution)/shard_map/dot_general | solution.py:15
  97.7 170.4 %reduce-scatter.2.cloned.1.call-done = f32[256,1024]{1,0:T(8,128)} async-done(((f32[4096,1024]{1,0:T(8,128)}), f32[256,1024]{1,0:T(8,128)}) %reduce-scatter.2.cloned.1.call-update) | async-done | bytes 1048592 | tf_op jit(solution)/shard_map/reduce_scatter | solution.py:23
  268.0 2.3 multiply_bitcast_fusion
Async XLA Ops:
  8.0 1.4 copy-start
  8.0 34.5 %all-reduce.2.cloned.1.call-start = ((), (), s32[]{:S(2)}) async-start(), calls=%async_computation.2 | async-start | bytes 1048576 | tf_op jit(solution)/shard_map/psum | solution.py:25
  8.7 79.4 %all-gather.3.cloned.1.call-start = ((), (), s32[]{:S(2)}) async-start(), calls=%async_computation.3 | async-start | bytes 8912896 | tf_op jit(solution)/shard_map/all_gather | solution.py:17
  9.3 258.7 %reduce-scatter.2.cloned.1.call-start = ((), (), s32[]{:S(2)}) async-start(), calls=%async_computation.1 | async-start | bytes 17825792 | tf_op jit(solution)/shard_map/reduce_scatter | solution.py:23
  20.0 22.6 %copy-start.1 = (f32[131072]{0:T(1024)S(1)}, f32[131072]{0:T(1024)}, u32[]{:S(2)}) copy-start(f32[131072]{0:T(1024)} %param.9) | copy-start | bytes 1572868
  20.0 22.6 %copy-start.2 = (f32[131072]{0:T(1024)S(1)}, f32[131072]{0:T(1024)}, u32[]{:S(2)}) copy-start(f32[131072]{0:T(1024)} %param.11) | copy-start | bytes 1572868
Sparse Core Ops, SparseCore 0:
  11.1 31.3 all-reduce.1
Sparse Core Ops, SparseCore 1:
  11.4 76.7 all-gather.2
  92.2 175.8 reduce-scatter.1
where the time goes:
time: 278 us
  waiting for transfers between devices  238 us (86%)
  matrix products  20 us (7%)
  between operations  15.5 us (6%)
  other arithmetic  4.49 us (2%)
    reduce_scatter x1, waiting for transfers between devices, shards(): lax.psum_scatter(grad_term(tokens, value_cot), 'fsdp', scatter_dimension=...  170 us
    all_gather x1, waiting for transfers between devices, shards(): lax.all_gather(weight, 'fsdp', axis=0, tiled=True)  43.5 us
    psum x1, waiting for transfers between devices, shards(): totals = lax.psum(local_params[0], 'rep')  22.5 us
    dot_general x1, matrix products, grad_term(): lax.dot_general(tokens, columns, (((0,), (0,)), ((), ())), preferred_elem...  10.6 us
    dot_general x1, matrix products, shards(): lax.dot_general(value_cot, lax.all_gather(weight, 'fsdp', axis=0, tiled=T...  9.45 us
  transfers between devices with their start and end apart: 3, of which 3 were waited for; matrix products, arithmetic and copies ran while one was open for 8% of the time, Pallas kernels for 0%

commit v1 on v0

--- a/solution.py
+++ b/solution.py
@@ -22,7 +22,7 @@
     factor = 1.0 / jnp.sqrt(jnp.float32(tokens.shape[0] * groups))
     summed = lax.psum_scatter(grad_term(tokens, value_cot), "fsdp", scatter_dimension=0, tiled=True)
     value_grad = (summed * factor)[None]
-    totals = lax.psum(local_params[0], "rep")
+    totals = jnp.sum(lax.all_gather(local_params[0], "rep"), axis=0)
     pseudo = global_params - totals / lax.axis_size("rep")
     new_moment = 0.9 * momentum + pseudo
     new_global = global_params - 0.7 * (pseudo + 0.9 * new_moment)

time: 278 us -> 299 us (1.076)
  waiting for transfers between devices: 238 us -> 259 us
    all_gather x1, waiting for transfers between devices: 43.5 us -> 72.6 us  [shards(): lax.all_gather(weight, 'fsdp', axis=0, tiled=True)]
    psum x1 -> x0, waiting for transfers between devices: 22.5 us -> none  [shards(): totals = lax.psum(local_params[0], 'rep')]
    all_gather x0 -> x1, waiting for transfers between devices: none -> 14.2 us  [shards(): totals = jnp.sum(lax.all_gather(local_params[0], 'rep'), axis=0)]
where the time goes in v1:
time: 299 us
  waiting for transfers between devices  259 us (87%)
  matrix products  20.1 us (7%)
  between operations  13.8 us (5%)
  other arithmetic  6.19 us (2%)
    reduce_scatter x1, waiting for transfers between devices, shards(): lax.psum_scatter(grad_term(tokens, value_cot), 'fsdp', scatter_dimension=...  171 us
    all_gather x1, waiting for transfers between devices, shards(): lax.all_gather(weight, 'fsdp', axis=0, tiled=True)  72.6 us
    all_gather x1, waiting for transfers between devices, shards(): totals = jnp.sum(lax.all_gather(local_params[0], 'rep'), axis=0)  14.2 us
    dot_general x1, matrix products, grad_term(): lax.dot_general(tokens, columns, (((0,), (0,)), ((), ())), preferred_elem...  10.6 us
    dot_general x1, matrix products, shards(): lax.dot_general(value_cot, lax.all_gather(weight, 'fsdp', axis=0, tiled=T...  9.45 us
  transfers between devices with their start and end apart: 3, of which 3 were waited for; matrix products, arithmetic and copies ran while one was open for 8% of the time, Pallas kernels for 0%

profile of v1, /device:TPU:0, one launch (start us, length us, event | category | flops | bytes accessed | tf_op | source)
XLA Modules:
  0.0 299.0 jit_solution(2547519507922141982)
XLA Ops:
  7.2 0.0 copy-start
  7.2 0.0 all-gather.7.cloned.1.call-start
  7.2 0.7 all-gather.7.cloned.1.call-update
  7.9 0.0 all-gather.5.cloned.1.call-start
  8.0 0.7 all-gather.5.cloned.1.call-update
  8.7 0.0 reduce-scatter.2.cloned.1.call-start
  8.7 0.0 copy-done
  8.7 10.6 %fusion.5 = f32[4096,1024]{1,0:T(8,128)} fusion(bf16[512,4096]{1,0:T(8,128)(2,1)} %param.6, bf16[512,1024]{1,0:T(8,128)(2,1)S(1)} %copy-done), kind=kOutput, calls=%fused_computation.7 | convolution fusion | flops 4294967296 | bytes 22020096 | tf_op jit(solution)/shard_map/dot_general | solution.py:8
  19.4 0.0 copy-start.1
  19.4 0.0 copy-start.2
  19.4 0.0 reduce-scatter.2.cloned.1.call-update
  19.4 14.2 %all-gather.7.cloned.1.call-done = f32[2,1,131072]{2,1,0:T(1,128)} async-done(((f32[1,1,131072]{2,1,0:T(1,128)}), f32[2,1,131072]{2,1,0:T(1,128)}) %all-gather.7.cloned.1.call-update) | async-done | bytes 1048592 | tf_op jit(solution)/shard_map/all_gather | solution.py:25
  33.6 2.7 reduce_sum.9
  36.3 0.0 copy-done.1
  36.3 0.0 copy-done.2
  36.3 1.1 multiply_subtract_fusion
  37.4 72.6 %all-gather.5.cloned.1.call-done = bf16[1,4096,1024]{2,1,0:T(8,128)(2,1)} async-done(((bf16[1,256,1024]{2,1,0:T(8,128)(2,1)}), bf16[1,4096,1024]{2,1,0:T(8,128)(2,1)}) %all-gather.5.cloned.1.call-update) | async-done | bytes 8388624 | tf_op jit(solution)/shard_map/all_gather | solution.py:17
  110.1 9.5 %fusion.2 = bf16[512,4096]{1,0:T(8,128)(2,1)} fusion(bf16[512,1024]{1,0:T(8,128)(2,1)S(1)} %copy-done, bf16[1,4096,1024]{2,1,0:T(8,128)(2,1)} %all-gather.5.cloned.1.call-done), kind=kOutput, calls=%fused_computation.2 | convolution fusion | flops 4297064448 | bytes 13631488 | tf_op jit(solution)/shard_map/dot_general | solution.py:15
  119.5 170.6 %reduce-scatter.2.cloned.1.call-done = f32[256,1024]{1,0:T(8,128)} async-done(((f32[4096,1024]{1,0:T(8,128)}), f32[256,1024]{1,0:T(8,128)}) %reduce-scatter.2.cloned.1.call-update) | async-done | bytes 1048592 | tf_op jit(solution)/shard_map/reduce_scatter | solution.py:23
  290.1 2.3 multiply_bitcast_fusion
Async XLA Ops:
  7.2 1.5 copy-start
  7.2 26.4 %all-gather.7.cloned.1.call-start = ((), (), s32[]{:S(2)}) async-start(), calls=%async_computation.3 | async-start | bytes 1572864 | tf_op jit(solution)/shard_map/all_gather | solution.py:25
  7.9 102.1 %all-gather.5.cloned.1.call-start = ((), (), s32[]{:S(2)}) async-start(), calls=%async_computation.2 | async-start | bytes 8912896 | tf_op jit(solution)/shard_map/all_gather | solution.py:17
  8.7 281.4 %reduce-scatter.2.cloned.1.call-start = ((), (), s32[]{:S(2)}) async-start(), calls=%async_computation.1 | async-start | bytes 17825792 | tf_op jit(solution)/shard_map/reduce_scatter | solution.py:23
  19.4 17.0 %copy-start.1 = (f32[131072]{0:T(1024)S(1)}, f32[131072]{0:T(1024)}, u32[]{:S(2)}) copy-start(f32[131072]{0:T(1024)} %param.9) | copy-start | bytes 1572868
  19.4 17.0 %copy-start.2 = (f32[131072]{0:T(1024)S(1)}, f32[131072]{0:T(1024)}, u32[]{:S(2)}) copy-start(f32[131072]{0:T(1024)} %param.11) | copy-start | bytes 1572868
Sparse Core Ops, SparseCore 0:
  9.5 23.9 all-gather.6
  35.7 74.2 all-gather.4
  114.2 175.8 reduce-scatter.1
